TPU v7x, 32 devices: a whole 2x2x4 slice. The times are simulated.
32 devices in a mesh: fsdp: 4 (over y, x), rep: 8 (over z, core).
Axes of the slice: x: 2, y: 2, z: 4, core: 2. Of those that a mesh axis runs over, the one named last changes fastest.
Arguments:
- hidden_in: bfloat16 [8192, 2048], P(('fsdp', 'rep'))
- out_grad: bfloat16 [8192, 2048], P(('fsdp', 'rep')), may hold values from -6 to 6
- attn_saved: bfloat16 [8192, 256], P(('fsdp', 'rep')), may hold values from -6 to 6
- row_lse: float32 [8192, 2], P(('fsdp', 'rep')), may hold values from 2.5 to 6
- w_qkv: bfloat16 [2048, 512], P('fsdp'), may hold values from -0.125 to 0.125
- w_out_t: bfloat16 [2048, 256], P('fsdp'), may hold values from -0.125 to 0.125
- doc_lengths: int32 [32, 4], P(('fsdp', 'rep')), may hold values from 1 to 128, 256 in all within a row
- seq_start: int32 [32], P(('fsdp', 'rep')), may hold values from 0 to 2047
Outputs:
- input_grad: bfloat16 [8192, 2048], P(('fsdp', 'rep'))
- grad_update: float32 [2048, 768], P('fsdp')
- grad_norm: float32 [], replicated
Inputs may be any that keep to these rules, and one draw needn't show every extreme that they name: `doc_lengths`: each row sums to 256; the longest document of each device has exactly 128 tokens.
All inputs are finite; a program needn't handle non-finite values.
Results may differ from a plain program's by a relative error of at most 0.014.
Values may be sent and summed in bfloat16 or wider, within the bound.
A program may use at most 64 MiB of HBM per device.

v0:
```python
import jax
import jax.numpy as jnp
from jax import lax
from jax.sharding import PartitionSpec as P

D = 2048
HEAD = 128


def rotary(values_in, positions, turn, head_size):
    rows = values_in.shape[0]
    heads_count = values_in.shape[1] // head_size
    half_size = head_size // 2
    inverse = 1000000.0 ** (-(jnp.arange(half_size, dtype=jnp.float32) * 2.0) / head_size)
    angles = positions.astype(jnp.float32)[:, None] * inverse[None, :]
    cosine = jnp.cos(angles)[:, None, :]
    sines = jnp.sin(angles)[:, None, :]
    shaped = values_in.reshape(rows, heads_count, head_size)
    first_half = shaped[:, :, :half_size]
    second_half = shaped[:, :, half_size:]
    result = jnp.concatenate(
        [
            first_half * cosine - turn * second_half * sines,
            second_half * cosine + turn * first_half * sines,
        ],
        axis=2,
    )
    return result.reshape(rows, heads_count * head_size)


def contract_rows(left, right):
    return lax.dot_general(
        left, right, (((0,), (0,)), ((), ())), preferred_element_type=jnp.float32
    )


def contract_cols(left, right):
    return lax.dot_general(
        left, right, (((1,), (1,)), ((), ())), preferred_element_type=jnp.float32
    )


def body(hidden_in, out_grad, attn_saved, row_lse, w_qkv, w_out_t, doc_lengths, seq_start):
    seq_rows = hidden_in.shape[0]
    head_size = HEAD
    query_width = attn_saved.shape[1]
    heads_count = row_lse.shape[1]
    scale = 1.0 / head_size**0.5
    tokens_part = hidden_in
    grads_part = out_grad
    proj = jnp.dot(
        tokens_part,
        lax.all_gather(w_qkv, "fsdp", axis=0, tiled=True),
        preferred_element_type=jnp.float32,
    )
    attn_full = jnp.dot(
        grads_part,
        lax.all_gather(w_out_t, "fsdp", axis=0, tiled=True),
        preferred_element_type=jnp.float32,
    )
    attn_grad = attn_full.astype(jnp.bfloat16)
    positions = seq_start[0] + jnp.arange(seq_rows, dtype=jnp.int32)
    queries = rotary(proj[:, :query_width], positions, 1.0, head_size).astype(jnp.bfloat16)
    keys = rotary(proj[:, query_width : query_width + head_size], positions, 1.0, head_size).astype(
        jnp.bfloat16
    )
    values_all = proj[:, query_width + head_size :].astype(jnp.bfloat16)
    ends = jnp.cumsum(doc_lengths[0])
    local_rows = jnp.arange(seq_rows, dtype=jnp.int32)
    documents = jnp.sum((local_rows[:, None] >= ends[None, :]).astype(jnp.int32), axis=1)
    block_rows = min(seq_rows, 512)
    block_count = seq_rows // block_rows

    def attend_block(carry, inputs):
        key_grad, value_grad = carry
        query_rows, grad_rows, saved_rows, lse_rows, index_rows, doc_rows = inputs
        allowed = (doc_rows[:, None] == documents[None, :]) & (
            local_rows[None, :] <= index_rows[:, None]
        )
        query_parts = []
        for head_index in range(heads_count):
            lower = head_index * head_size
            query_head = query_rows[:, lower : lower + head_size]
            scores = contract_cols(query_head, keys) * scale
            probs = jnp.where(
                allowed, jnp.exp(scores - lse_rows[:, head_index : head_index + 1]), 0.0
            )
            grad_head = grad_rows[:, lower : lower + head_size]
            dprobs = contract_cols(grad_head, values_all)
            delta = jnp.sum(
                grad_head.astype(jnp.float32)
                * saved_rows[:, lower : lower + head_size].astype(jnp.float32),
                axis=1,
                keepdims=True,
            )
            dscores = (probs * (dprobs - delta) * scale).astype(jnp.bfloat16)
            probs_low = probs.astype(jnp.bfloat16)
            value_grad = value_grad + contract_rows(probs_low, grad_head)
            query_parts.append(jnp.dot(dscores, keys, preferred_element_type=jnp.float32))
            key_grad = key_grad + contract_rows(dscores, query_head)
        return ((key_grad, value_grad), jnp.concatenate(query_parts, axis=1))

    block_inputs = (
        queries.reshape(block_count, block_rows, query_width),
        attn_grad.reshape(block_count, block_rows, query_width),
        attn_saved.reshape(block_count, block_rows, query_width),
        row_lse.reshape(block_count, block_rows, heads_count),
        local_rows.reshape(block_count, block_rows),
        documents.reshape(block_count, block_rows),
    )
    zero_grad = jnp.zeros((seq_rows, head_size), jnp.float32)
    (key_grad, value_grad), query_blocks = lax.scan(
        attend_block, (zero_grad, zero_grad), block_inputs
    )
    query_grad = rotary(
        query_blocks.reshape(seq_rows, query_width), positions, -1.0, head_size
    ).astype(jnp.bfloat16)
    key_grad = rotary(key_grad, positions, -1.0, head_size).astype(jnp.bfloat16)
    d_qkv = jnp.concatenate([query_grad, key_grad, value_grad.astype(jnp.bfloat16)], axis=1)
    input_full = contract_cols(d_qkv, lax.all_gather(w_qkv, "fsdp", axis=0, tiled=True))
    input_grad = input_full.astype(jnp.bfloat16)
    tokens_part = hidden_in
    grads_part = out_grad
    shard_sum = lax.psum_scatter(
        jnp.concatenate(
            [contract_rows(tokens_part, d_qkv), contract_rows(grads_part, attn_saved)], axis=1
        ).astype(jnp.bfloat16),
        "fsdp",
        scatter_dimension=0,
        tiled=True,
    ).astype(jnp.float32)
    grads = lax.psum(shard_sum, "rep")
    norm_sq = lax.psum(jnp.sum(grads * grads), "fsdp")
    grad_update = grads * lax.rsqrt(norm_sq / (D * grads.shape[1]) + 1e-06)
    return (input_grad, grad_update, jnp.sqrt(norm_sq))


def solution(mesh):
    in_specs = (
        P(("fsdp", "rep"), None),
        P(("fsdp", "rep"), None),
        P(("fsdp", "rep"), None),
        P(("fsdp", "rep"), None),
        P("fsdp", None),
        P("fsdp", None),
        P(("fsdp", "rep"), None),
        P(("fsdp", "rep")),
    )
    out_specs = (P(("fsdp", "rep"), None), P("fsdp", None), P())
    return jax.shard_map(body, mesh=mesh, in_specs=in_specs, out_specs=out_specs, check_vma=False)
```

profile of v0, /device:TPU:0, one launch (start us, length us, event | category | flops | bytes accessed | tf_op | source)
XLA Modules:
  0.0 219.8 jit_solution(17886597577698370556)
XLA Ops:
  7.2 0.7 all-gather.5.cloned.1.call-update
  8.0 0.7 all-gather.3.cloned.1.call-update
  9.4 0.9 fusion.49
  10.3 0.7 copy.36
  11.0 0.7 copy.37
  11.7 0.8 reduce-window.8
  12.6 0.7 convert_reduce_fusion
  13.2 1.3 fusion.50
  14.6 1.2 broadcast_multiply_fusion.1
  15.8 1.4 convolution_convert_fusion.2
  17.2 21.9 %all-gather.5.cloned.1.call-done = bf16[2048,256]{1,0:T(8,128)(2,1)} async-done(((bf16[512,256]{1,0:T(8,128)(2,1)}), bf16[2048,256]{1,0:T(8,128)(2,1)}) %all-gather.5.cloned.1.call-update) | async-done | bytes 1048592 | tf_op jit(solution)/shard_map/all_gather | solution.py:58
  39.1 1.7 convolution_convert_fusion.3
  40.8 0.9 multiply_reduce_fusion.1
  41.8 34.4 %all-gather.3.cloned.1.call-done = bf16[2048,512]{1,0:T(8,128)(2,1)} async-done(((bf16[512,512]{1,0:T(8,128)(2,1)}), bf16[2048,512]{1,0:T(8,128)(2,1)}) %all-gather.3.cloned.1.call-update) | async-done | bytes 2097168 | tf_op jit(solution)/shard_map/all_gather | solution.py:53
  76.1 2.3 %fusion.51 = f32[256,512]{1,0:T(8,128)S(1)} fusion(bf16[256,2048]{1,0:T(8,128)(2,1)S(1)} %copy-done, bf16[2048,512]{1,0:T(8,128)(2,1)} %all-gather.3.cloned.1.call-done), kind=kOutput, calls=%fused_computation.89 | convolution fusion | flops 536870912 | bytes 3670016 | tf_op jit(solution)/shard_map/dot_general | solution.py:51
  78.6 1.0 fusion.28
  79.7 0.5 subtract_convert_fusion.1
  80.2 0.4 pad_maximum_fusion.3
  80.6 1.0 fusion.10
  83.4 0.2 fusion.13
  83.6 0.3 fusion.32
  84.4 1.2 subtract_convert_fusion
  85.6 0.4 pad_maximum_fusion.4
  86.0 0.7 fusion
  86.7 1.9 pad_maximum_fusion
  88.7 44.1 %reduce-scatter.2.cloned.1.call-done = bf16[512,768]{0,1:T(8,128)(2,1)} async-done(((bf16[2048,768]{0,1:T(8,128)(2,1)}), bf16[512,768]{0,1:T(8,128)(2,1)}) %reduce-scatter.2.cloned.1.call-update) | async-done | bytes 786448 | tf_op jit(solution)/shard_map/reduce_scatter | solution.py:124
  132.7 59.9 %all-reduce.1 = f32[512,768]{0,1:T(8,128)S(1)} all-reduce(bf16[512,768]{0,1:T(8,128)(2,1)} %reduce-scatter.2.cloned.1.call-done), channel_id=1, replica_groups=mesh['fsdp'=4,'rep'=8] {'rep'}, use_global_device_ids=true, to_apply=%region_5.6 | all-reduce | flops 393216 | bytes 2359296 | tf_op jit(solution)/shard_map/psum | solution.py:132
  192.6 1.0 multiply_reduce_fusion
  193.6 3.3 %convolution_convert_fusion.1 = bf16[256,2048]{1,0:T(8,128)(2,1)} fusion(bf16[2048,512]{1,0:T(8,128)(2,1)} %all-gather.3.cloned.1.call-done, bf16[256,128]{1,0:T(8,128)(2,1)S(1)} %copy.33, bf16[256,128]{1,0:T(8,128)(2,1)S(1)} %copy.32, bf16[256,256]{1,0:T(8,128)(2,1)S(1)} %bitcast.49), kind=kOutput, calls=%fused_computation.3 | convolution fusion | flops 538181632 | bytes 3407872 | tf_op jit(solution)/shard_map/dot_general | solution.py:38
  196.9 9.5 %psum.15 = f32[]{:T(128)} all-reduce(f32[]{:T(128)} %multiply_reduce_fusion), channel_id=1, replica_groups=mesh['fsdp'=4,'rep'=8] {'fsdp'}, use_global_device_ids=true, to_apply=%region_7.8 | all-reduce | flops 1 | bytes 8 | tf_op jit(solution)/shard_map/psum | solution.py:133
  207.8 1.3 broadcast_multiply_fusion
  209.1 3.0 %copy.34 = f32[512,768]{1,0:T(8,128)} copy(f32[512,768]{0,1:T(8,128)} %broadcast_multiply_fusion) | data formatting | bytes 3145728
  (39 shorter events, 2.6 us)
Async XLA Ops:
  7.2 69.0 %copy-start = (bf16[256,2048]{1,0:T(8,128)(2,1)S(1)}, bf16[256,2048]{1,0:T(8,128)(2,1)}, u32[]{:S(2)}) copy-start(bf16[256,2048]{1,0:T(8,128)(2,1)} %param.8) | copy-start | bytes 3145732
  7.2 8.6 %copy-start.1 = (bf16[256,2048]{1,0:T(8,128)(2,1)S(1)}, bf16[256,2048]{1,0:T(8,128)(2,1)}, u32[]{:S(2)}) copy-start(bf16[256,2048]{1,0:T(8,128)(2,1)} %param.9) | copy-start | bytes 3145732
  7.2 31.9 %all-gather.5.cloned.1.call-start = ((), (), s32[]{:S(2)}) async-start(), calls=%async_computation.2 | async-start | bytes 1310720 | tf_op jit(solution)/shard_map/all_gather | solution.py:58
  7.9 68.2 %all-gather.3.cloned.1.call-start = ((), (), s32[]{:S(2)}) async-start(), calls=%async_computation.1 | async-start | bytes 2621440 | tf_op jit(solution)/shard_map/all_gather | solution.py:53
  8.7 124.0 %reduce-scatter.2.cloned.1.call-start = ((), (), s32[]{:S(2)}) async-start(), calls=%async_computation.3 | async-start | bytes 3932160 | tf_op jit(solution)/shard_map/reduce_scatter | solution.py:124
  79.7 2.3 %copy-start.2 = (bf16[256,1,64]{0,2,1:T(8,128)(2,1)S(1)}, bf16[256,1,64]{0,2,1:T(8,128)(2,1)}, u32[]{:S(2)}) copy-start(bf16[256,1,64]{0,2,1:T(8,128)(2,1)} %get-tuple-element.64) | copy-start | bytes 98308
  79.7 2.3 %copy-start.3 = (bf16[256,1,64]{0,2,1:T(8,128)(2,1)S(1)}, bf16[256,1,64]{0,2,1:T(8,128)(2,1)}, u32[]{:S(2)}) copy-start(bf16[256,1,64]{0,2,1:T(8,128)(2,1)} %get-tuple-element.65) | copy-start | bytes 98308
  79.7 2.7 %copy-start.4 = (f32[256,1]{0,1:T(1,128)S(1)}, f32[256,1]{0,1:T(1,128)}, u32[]{:S(2)}) copy-start(f32[256,1]{0,1:T(1,128)} %get-tuple-element.68) | copy-start | bytes 3076
  79.7 2.7 %copy-start.5 = (s32[256]{0:T(256)S(1)}, s32[256]{0:T(256)}, u32[]{:S(2)}) copy-start(s32[256]{0:T(256)} %convert_reduce_fusion) | copy-start | bytes 3076
Sparse Core Ops, SparseCore 0:
  9.8 29.2 all-gather.4
  40.9 35.1 all-gather.2
  88.8 43.8 reduce-scatter.1
where the time goes:
time: 220 us
  waiting for transfers between devices  102 us (46%)
  blocking collectives  69.4 us (32%)
  between operations  17.2 us (8%)
  matrix products  12.2 us (6%)
  other arithmetic  11.5 us (5%)
  local copies, waits for them, and re-layouts  7.61 us (3%)
    psum x1, blocking collectives, body(): grads = lax.psum(shard_sum, 'rep')  59.9 us
    reduce_scatter x1, waiting for transfers between devices, body(): lax.psum_scatter(jnp.concatenate([contract_rows(tokens_part, d_qkv), cont...  44.1 us
    all_gather x1, waiting for transfers between devices, body(): lax.all_gather(w_qkv, 'fsdp', axis=0, tiled=True)  34.4 us
    all_gather x1, waiting for transfers between devices, body(): lax.all_gather(w_out_t, 'fsdp', axis=0, tiled=True)  21.9 us
    psum x1, blocking collectives, body(): norm_sq = lax.psum(jnp.sum(grads * grads), 'fsdp')  9.53 us
    unnamed x20, local copies, waits for them, and re-layouts  4.97 us
    dot_general x5, matrix products, contract_cols(): lax.dot_general(left, right, (((1,), (1,)), ((), ())), preferred_element_...  4.91 us
  transfers between devices with their start and end apart: 3, of which 3 were waited for; matrix products, arithmetic and copies ran while one was open for 5% of the time, Pallas kernels for 0%

commit v1 on v0

v1 whole, which is shorter than its diff:
```python
import functools

import jax
import jax.numpy as jnp
import numpy as np
from jax import lax
from jax.experimental import pallas as pl
from jax.experimental.pallas import tpu as pltpu
from jax.sharding import PartitionSpec as P

HEAD = 128
MESH = pl.DeviceIdType.MESH
F32, BF16 = jnp.float32, jnp.bfloat16


def dot(a, b, ca, cb):
    return lax.dot_general(a, b, (((ca,), (cb,)), ((), ())), preferred_element_type=F32)


def flip(index, bit):
    return index + bit * (1 - 2 * ((index // bit) % 2))


def kernel(
    n_fsdp, n_rep,
    hid_hbm, og_hbm, sav_hbm, lse_hbm, wq_hbm, wo_hbm, len_ref, start_ref, freq_ref,
    ig_hbm, gu_hbm, norm_ref,
    hid, og, sav, lse, wq, wo, hid_t, og_t, proj, ag, dqkv, ig, gu,
    part, core_in, rs_in, z_mid, z_in, fin, norms, tab,
    load_sem, out_sem,
    wq_send, wq_recv, wo_send, wo_recv, wqc_send, wqc_recv, woc_send, woc_recv,
    core_send, core_recv, rs_send, rs_recv, z_send, z_recv, fin_send, fin_recv,
    norm_send, norm_recv,
):
    f = lax.axis_index("fsdp")
    r = lax.axis_index("rep")
    core, z = r % 2, r // 2
    n_z = n_rep // 2
    nb = n_fsdp.bit_length() - 1
    seq = hid.shape[0]
    chunks, _, _, half, cw = part.shape
    heads = lse.shape[1]
    qw = heads * HEAD
    wr = 2 * half
    scale = 1.0 / HEAD**0.5
    partner = (f, r + 1 - 2 * core)

    loads = []
    for k, (src, dst) in enumerate(
        [(wo_hbm, wo.at[f]), (wq_hbm, wq.at[f]), (og_hbm, og), (sav_hbm, sav), (hid_hbm, hid), (lse_hbm, lse)]
    ):
        copy = pltpu.make_async_copy(src, dst, load_sem.at[k])
        copy.start()
        loads.append(copy)

    z_near = z + 1 - 2 * (z % 2)
    z_mirror = (z // 4) * 4 + 3 - z % 4
    z_far = []
    bit = 4
    while bit < n_z:
        z_far.append(flip(z, bit))
        bit *= 2
    barrier = pltpu.get_barrier_semaphore()
    greet = [partner]
    greet += [((f + k) % n_fsdp, r) for k in range(1, n_fsdp)]
    greet += [(f, 2 * peer + core) for peer in [z_near, z_mirror] + z_far]
    for peer in greet:
        pl.semaphore_signal(barrier, inc=1, device_id=peer, device_id_type=MESH)
    pl.semaphore_wait(barrier, len(greet))

    def remote(src, dst, send, recv, device):
        return pltpu.make_async_remote_copy(
            src_ref=src, dst_ref=dst, send_sem=send, recv_sem=recv, device_id=device, device_id_type=MESH
        )

    sent = []

    def go(copy):
        copy.start()
        sent.append(copy)

    bits = [(1 - core) * (1 << s) + core * (1 << (nb - 1 - s)) for s in range(nb)]
    near = [(flip(f, b), r) for b in bits]

    def block_of(mask):
        g = f
        for s in range(nb):
            if (mask >> s) & 1:
                g = flip(g, bits[s])
        return g

    def mirror(mask):
        return sum(1 << (nb - 1 - s) for s in range(nb) if (mask >> s) & 1)

    def weight_copies(mask, message, device):
        g = block_of(mask)
        return [
            remote(ref.at[g, core], ref.at[g, core], send.at[message], recv.at[message], device)
            for ref, send, recv in ((wo, wo_send, wo_recv), (wq, wq_send, wq_recv))
        ]

    def forward(mask):
        top = mask.bit_length()
        for s in range(top, nb):
            for copy in weight_copies(mask, mask | (1 << s), near[s]):
                go(copy)

    loads[0].wait()
    loads[1].wait()
    forward(0)

    rows = lax.broadcasted_iota(jnp.int32, (seq, HEAD), 0)
    angles = (rows + start_ref[0]).astype(F32) * freq_ref[0:1, :]
    tab[0] = jnp.cos(angles)
    lanes = lax.broadcasted_iota(jnp.int32, (seq, HEAD), 1)
    sines = jnp.sin(angles)
    tab[1] = jnp.where(lanes < HEAD // 2, -sines, sines)

    def rot(v, turn):
        turned = jnp.concatenate([v[:, HEAD // 2 :], v[:, : HEAD // 2]], axis=1)
        return v * tab[0] + turn * (turned * tab[1])

    loads[2].wait()
    loads[3].wait()
    for g in range(n_fsdp):
        block = og[:, g * wr : (g + 1) * wr].T
        og_t[g, 0] = block[:half]
        og_t[g, 1] = block[half:]

    def half_for_partner(chunk, left_t, right):
        for g in range(n_fsdp):
            part[chunk, 1 - core, g] = dot(left_t[g, 1 - core], right, 1, 0).astype(BF16)
        go(remote(part.at[chunk, 1 - core], core_in.at[chunk], core_send.at[chunk], core_recv.at[chunk], partner))

    def rs_copy(chunk, mask):
        low = (mask & -mask).bit_length() - 1
        g = block_of(mask)
        return remote(
            part.at[chunk, core, g], rs_in.at[chunk, mask], rs_send.at[chunk, mask], rs_recv.at[chunk, mask], near[low]
        )

    def own_half(chunk, left_t, right):
        remote(
            part.at[chunk, 1 - core], core_in.at[chunk], core_send.at[chunk], core_recv.at[chunk], partner
        ).wait_recv()
        order = sorted(range(n_fsdp), key=lambda m: 1 - m % 2)
        for mask in order:
            g = block_of(mask)
            part[chunk, core, g] = (dot(left_t[g, core], right, 1, 0) + core_in[chunk, g].astype(F32)).astype(BF16)
            if mask & 1:
                go(rs_copy(chunk, mask))

    def rs_stage(chunk, s):
        later = [m for m in range(n_fsdp) if m % (1 << (s + 1)) == 0]
        later = sorted(later, key=lambda m: 1 - (m >> (s + 1)) % 2)
        for mask in later:
            message = mask | (1 << s)
            rs_copy(chunk, message).wait_recv()
            g = block_of(mask)
            part[chunk, core, g] = (part[chunk, core, g].astype(F32) + rs_in[chunk, message].astype(F32)).astype(BF16)
            if (mask >> (s + 1)) & 1:
                go(rs_copy(chunk, mask))

    middle = ((z % 4) + 1) // 2 % 2 == 1
    z_dev = [(f, 2 * peer + core) for peer in [z_near, z_mirror] + z_far]

    def z_up(chunk):
        return remote(part.at[chunk, core, f], z_in.at[chunk, 0], z_send.at[chunk, 0], z_recv.at[chunk, 0], z_dev[0])

    def z_across(chunk, k):
        return remote(
            z_mid.at[chunk, k], z_in.at[chunk, k + 1], z_send.at[chunk, k + 1], z_recv.at[chunk, k + 1], z_dev[k + 1]
        )

    n_across = 1 + len(z_far)

    def z_down(chunk):
        k = n_across + 1
        return remote(fin.at[chunk, core], fin.at[chunk, core], z_send.at[chunk, k], z_recv.at[chunk, k], z_dev[0])

    def fin_copy(chunk):
        return remote(fin.at[chunk, core], fin.at[chunk, core], fin_send.at[chunk], fin_recv.at[chunk], partner)

    def fin_from_partner(chunk):
        return remote(fin.at[chunk, 1 - core], fin.at[chunk, 1 - core], fin_send.at[chunk], fin_recv.at[chunk], partner)

    def z_first(chunk):
        @pl.when(middle)
        def _():
            z_up(chunk).wait_recv()
            z_mid[chunk, 0] = (part[chunk, core, f].astype(F32) + z_in[chunk, 0].astype(F32)).astype(BF16)
            z_across(chunk, 0).start()

        @pl.when(jnp.logical_not(middle))
        def _():
            z_up(chunk).start()

    def z_second(chunk):
        @pl.when(middle)
        def _():
            for k in range(n_across):
                z_across(chunk, k).wait_recv()
                total = (z_mid[chunk, k].astype(F32) + z_in[chunk, k + 1].astype(F32)).astype(BF16)
                if k + 1 < n_across:
                    z_mid[chunk, k + 1] = total
                    z_across(chunk, k + 1).start()
                else:
                    fin[chunk, core] = total
            z_down(chunk).start()

    def z_third(chunk):
        @pl.when(jnp.logical_not(middle))
        def _():
            z_down(chunk).wait_recv()

        go(fin_copy(chunk))

    def z_drain(chunk):
        @pl.when(middle)
        def _():
            for k in range(n_across):
                z_across(chunk, k).wait_send()
            z_down(chunk).wait_send()

        @pl.when(jnp.logical_not(middle))
        def _():
            z_up(chunk).wait_send()

    half_for_partner(0, og_t, sav[...])
    loads[4].wait()
    loads[5].wait()
    for g in range(n_fsdp):
        block = hid[:, g * wr : (g + 1) * wr].T
        hid_t[g, 0] = block[:half]
        hid_t[g, 1] = block[half:]

    def project(mask, first):
        g = block_of(mask)
        columns = pl.ds(pl.multiple_of(g * wr, wr), wr)
        left, other = hid[:, columns], og[:, columns]
        new = dot(left, wq[g].reshape(wr, -1), 1, 0)
        new_ag = dot(other, wo[g].reshape(wr, -1), 1, 0)
        if first:
            proj[...] = new
            ag[...] = new_ag
        else:
            proj[...] += new
            ag[...] += new_ag

    project(0, True)

    def core_copies(mask, message, side):
        g = block_of(mask)
        return [
            remote(ref.at[g, side], ref.at[g, side], send.at[message], recv.at[message], partner)
            for ref, send, recv in ((wo, woc_send, woc_recv), (wq, wqc_send, wqc_recv))
        ]

    def arrive(mask):
        top = mask.bit_length() - 1
        for copy in weight_copies(mask, mask, near[top]):
            copy.wait_recv()
        forward(mask)
        for copy in core_copies(mask, mask, core):
            go(copy)

    def use(mask):
        for copy in core_copies(mask, mirror(mask), 1 - core):
            copy.wait_recv()
        project(mask, False)

    last = n_fsdp - 1
    for mask in range(1, last):
        arrive(mask)
    for mask in range(1, last):
        use(mask)
    own_half(0, og_t, sav[...])
    arrive(last)
    use(last)

    queries = [rot(proj[:, h * HEAD : (h + 1) * HEAD], 1.0).astype(BF16) for h in range(heads)]
    keys = rot(proj[:, qw : qw + HEAD], 1.0).astype(BF16)
    values = proj[:, qw + HEAD :].astype(BF16)

    def documents(shape, axis):
        at = lax.broadcasted_iota(jnp.int32, shape, axis)
        count, end = jnp.zeros(shape, jnp.int32), 0
        for k in range(len_ref.shape[1]):
            end = end + len_ref[0, k]
            count = count + (at >= end).astype(jnp.int32)
        return at, count

    row_at, row_doc = documents((seq, seq), 0)
    col_at, col_doc = documents((seq, seq), 1)
    allowed = (row_doc == col_doc) & (col_at <= row_at)
    key_grad = jnp.zeros((seq, HEAD), F32)
    value_grad = jnp.zeros((seq, HEAD), F32)
    for h in range(heads):
        lanes_h = slice(h * HEAD, (h + 1) * HEAD)
        scores = dot(queries[h], keys, 1, 1) * scale
        probs = jnp.where(allowed, jnp.exp(scores - lse[:, h : h + 1]), 0.0)
        grad_head = ag[:, lanes_h].astype(BF16)
        dprobs = dot(grad_head, values, 1, 1)
        delta = jnp.sum(grad_head.astype(F32) * sav[:, lanes_h].astype(F32), axis=1, keepdims=True)
        dscores = (probs * (dprobs - delta) * scale).astype(BF16)
        value_grad = value_grad + dot(probs.astype(BF16), grad_head, 0, 0)
        key_grad = key_grad + dot(dscores, queries[h], 0, 0)
        dqkv[:, lanes_h] = rot(dot(dscores, keys, 1, 0), -1.0).astype(BF16)
        if h < nb:
            rs_stage(0, h)
    dqkv[:, qw : qw + HEAD] = rot(key_grad, -1.0).astype(BF16)
    dqkv[:, qw + HEAD :] = value_grad.astype(BF16)

    rest = list(range(1, chunks))
    right_of = {c: dqkv[:, (c - 1) * cw : c * cw] for c in rest}
    for c in rest:
        half_for_partner(c, hid_t, right_of[c])
    for c in rest:
        own_half(c, hid_t, right_of[c])
    for s in range(heads, nb):
        rs_stage(0, s)
    z_first(0)

    def grad_block(g):
        columns = slice(g * wr, (g + 1) * wr)
        ig[:, columns] = dot(dqkv[...], wq[g].reshape(wr, -1), 1, 1).astype(BF16)

    for g in range(n_fsdp // 2):
        grad_block(g)
    z_second(0)
    for g in range(n_fsdp // 2, n_fsdp):
        grad_block(g)
    ig_out = pltpu.make_async_copy(ig, ig_hbm, out_sem.at[0])
    ig_out.start()
    z_third(0)
    for s in range(nb):
        for c in rest:
            rs_stage(c, s)
            if s == nb - 1:
                z_first(c)
    for c in rest:
        z_second(c)
    for c in rest:
        z_third(c)

    squares = jnp.zeros((half, cw), F32)
    for c in range(chunks):
        fin_from_partner(c).wait_recv()
        low, high = fin[c, 0].astype(F32), fin[c, 1].astype(F32)
        squares = squares + low * low + high * high
    mine = jnp.sum(jnp.sum(squares, axis=0, keepdims=True), axis=1, keepdims=True)
    norms[f] = jnp.broadcast_to(mine, norms.shape[1:])
    for k in range(1, n_fsdp):
        go(remote(norms.at[f], norms.at[f], norm_send.at[k], norm_recv.at[k], ((f + k) % n_fsdp, r)))
    for k in range(1, n_fsdp):
        origin = (f + n_fsdp - k) % n_fsdp
        remote(norms.at[origin], norms.at[origin], norm_send.at[k], norm_recv.at[k], (origin, r)).wait_recv()
    total = norms[0]
    for g in range(1, n_fsdp):
        total = total + norms[g]
    norm_ref[...] = jnp.sqrt(total)
    size = n_fsdp * wr * chunks * cw
    factor = lax.rsqrt(total[0:1, 0:1] / size + 1e-06)
    for c in range(chunks):
        at = (c - 1) % chunks * cw
        for side in range(2):
            gu[side * half : (side + 1) * half, at : at + cw] = fin[c, side].astype(F32) * factor
    gu_out = pltpu.make_async_copy(gu, gu_hbm, out_sem.at[1])
    gu_out.start()
    for copy in sent:
        copy.wait_send()
    for c in range(chunks):
        z_drain(c)
    ig_out.wait()
    gu_out.wait()


def solution(mesh):
    n_fsdp, n_rep = mesh.shape["fsdp"], mesh.shape["rep"]

    def body(hidden_in, out_grad, attn_saved, row_lse, w_qkv, w_out_t, doc_lengths, seq_start):
        seq, width = hidden_in.shape
        qw, cols = attn_saved.shape[1], w_qkv.shape[1]
        wr = w_qkv.shape[0]
        half, cw = wr // 2, qw
        chunks = 1 + cols // cw
        n_across = (n_rep // 2).bit_length() - 2
        lane = np.arange(HEAD) % (HEAD // 2)
        freq = np.broadcast_to((1000000.0 ** (-2.0 * lane / HEAD)).astype(np.float32), (8, HEAD))
        dma = pltpu.SemaphoreType.DMA
        anywhere = pl.BlockSpec(memory_space=pl.ANY)
        scalar = pl.BlockSpec(memory_space=pltpu.SMEM)
        vmem = pl.BlockSpec(memory_space=pltpu.VMEM)
        F = n_fsdp
        ig, gu, norm = pl.pallas_call(
            functools.partial(kernel, n_fsdp, n_rep),
            out_shape=(
                jax.ShapeDtypeStruct((seq, width), BF16),
                jax.ShapeDtypeStruct((wr, chunks * cw), F32),
                jax.ShapeDtypeStruct((8, 128), F32),
            ),
            in_specs=[anywhere] * 6 + [scalar] * 2 + [vmem],
            out_specs=(anywhere, anywhere, vmem),
            scratch_shapes=[
                pltpu.VMEM((seq, width), BF16),
                pltpu.VMEM((seq, width), BF16),
                pltpu.VMEM((seq, qw), BF16),
                pltpu.VMEM(row_lse.shape, F32),
                pltpu.VMEM((F, 2, half, cols), BF16),
                pltpu.VMEM((F, 2, half, qw), BF16),
                pltpu.VMEM((F, 2, half, seq), BF16),
                pltpu.VMEM((F, 2, half, seq), BF16),
                pltpu.VMEM((seq, cols), F32),
                pltpu.VMEM((seq, qw), F32),
                pltpu.VMEM((seq, cols), BF16),
                pltpu.VMEM((seq, width), BF16),
                pltpu.VMEM((wr, chunks * cw), F32),
                pltpu.VMEM((chunks, 2, F, half, cw), BF16),
                pltpu.VMEM((chunks, F, half, cw), BF16),
                pltpu.VMEM((chunks, F, half, cw), BF16),
                pltpu.VMEM((chunks, n_across, half, cw), BF16),
                pltpu.VMEM((chunks, n_across + 1, half, cw), BF16),
                pltpu.VMEM((chunks, 2, half, cw), BF16),
                pltpu.VMEM((F, 8, 128), F32),
                pltpu.VMEM((2, seq, HEAD), F32),
                dma((6,)),
                dma((2,)),
            ]
            + [dma((F,))] * 8
            + [dma((chunks,))] * 2
            + [dma((chunks, F))] * 2
            + [dma((chunks, n_across + 2))] * 2
            + [dma((chunks,))] * 2
            + [dma((F,))] * 2,
            compiler_params=pltpu.CompilerParams(
                collective_id=0, has_side_effects=True, vmem_limit_bytes=56 * 2**20
            ),
        )(
            hidden_in, out_grad, attn_saved, row_lse,
            w_qkv.reshape(2, half, cols), w_out_t.reshape(2, half, qw),
            doc_lengths, seq_start, freq,
        )
        return ig, gu, norm[0, 0]

    rows = P(("fsdp", "rep"), None)
    in_specs = (rows, rows, rows, rows, P("fsdp", None), P("fsdp", None), rows, P(("fsdp", "rep")))
    return jax.shard_map(
        body, mesh=mesh, in_specs=in_specs, out_specs=(rows, P("fsdp", None), P()), check_vma=False
    )
```

time: 220 us -> 82.1 us (0.37)
  waiting for transfers between devices: 102 us -> 0 us
  Pallas kernels: 0 us -> 73 us
  blocking collectives: 69.4 us -> 0 us
  between operations: 17.2 us -> 1.3 us
  matrix products: 12.2 us -> 0 us
  other arithmetic: 11.5 us -> 0 us
    pallas_call x0 -> x1, Pallas kernels: none -> 73 us  [body(): pl.pallas_call(functools.partial(kernel, n_fsdp, n_rep), out_shape=(jax.S...]
    psum x2 -> x0, blocking collectives: 69.4 us -> none  [the longest x1 59.9 us: body(): grads = lax.psum(shard_sum, 'rep')]
    all_gather x2 -> x0, waiting for transfers between devices: 56.3 us -> none  [the longest x1 34.4 us: body(): lax.all_gather(w_qkv, 'fsdp', axis=0, tiled=True)]
    reduce_scatter x1 -> x0, waiting for transfers between devices: 44.1 us -> none  [body(): lax.psum_scatter(jnp.concatenate([contract_rows(tokens_part, d_qkv), cont...]
    dot_general x15 -> x0, matrix products: 12.2 us -> none  [the longest x5 4.91 us: contract_cols(): lax.dot_general(left, right, (((1,), (1,)), ((), ())), preferred_element_...]
    another operation x5 -> x0, other arithmetic: 3.76 us -> none
    concatenate x4 -> x0, other arithmetic: 2.62 us -> none  [the longest x1 1.88 us: body(): jnp.concatenate([contract_rows(tokens_part, d_qkv), contract_rows(grads_p...]
    reduce_sum x3 -> x0, other arithmetic: 2.59 us -> none  [the longest x1 1 us: body(): norm_sq = lax.psum(jnp.sum(grads * grads), 'fsdp')]
  transfers between devices with their start and end apart: 3 -> 0, of which waited for: 3 -> 0; matrix products, arithmetic and copies ran while one was open for 5% -> 0% of each run, Pallas kernels for 0% -> 0%
where the time goes in v1:
time: 82.1 us; the launch traced here: 81.8 us
  Pallas kernels  73 us (89%)
  local copies, waits for them, and re-layouts  7.48 us (9%)
  between operations  1.3 us (2%)
    pallas_call x1, Pallas kernels, body(): pl.pallas_call(functools.partial(kernel, n_fsdp, n_rep), out_shape=(jax.S...  73 us
    unnamed x5, local copies, waits for them, and re-layouts  4.93 us

profile of v1, /device:TPU:0, one launch (start us, length us, event | category | flops | bytes accessed | tf_op | source)
XLA Modules:
  0.0 81.8 jit_solution(13449189934030993643)
XLA Ops:
  1.3 1.5 %copy.12.lse_hbm = f32[256,2]{1,0:T(8,128)} copy(f32[256,2]{0,1:T(2,128)} %param.12) | data formatting | bytes 4096 | tf_op args[3]
  2.8 1.2 %jit_solution_.3.freq_ref = f32[8,128]{1,0:T(8,128)} broadcast(f32[128]{0:T(128)} %constant.2.clone), dimensions={1} | broadcast | bytes 4608 | tf_op jit(solution)
  4.0 73.0 %shard_map.112 = (bf16[256,2048]{1,0:T(8,128)(2,1)}, f32[512,768]{1,0:T(8,128)}, f32[8,128]{1,0:T(8,128)}) custom-call(bf16[256,2048]{1,0:T(8,128)(2,1)} %hid_hbm.1, bf16[256,2048]{1,0:T(8,128)(2,1)} %og_hbm.1, bf16[256,256]{1,0:T(8,128)(2,1)} %sav_hbm.1, f32[256,2]{1,0:T(8,128)} %copy.12.lse_hbm, bf16[2,256,512]{2,1,0:T(8,128)(2,1)} %bitcast.3, ...), custom_call_target="tpu_custom_call" | custom-call | tf_op jit(solution)/shard_map/pallas_call | solution.py:395
  77.1 0.0 copy-start
  77.1 1.3 %slice.3 = f32[1,1]{1,0:T(1,128)} slice(f32[8,128]{1,0:T(8,128)} %get-tuple-element.8), slice={[0:1], [0:1]} | slice | bytes 8 | tf_op jit(solution)/shard_map/slice | solution.py:443
  78.4 2.3 %copy.16 = bf16[256,2048]{1,0:T(8,128)(2,1)} copy(bf16[256,2048]{1,0:T(8,128)(2,1)} %get-tuple-element.12) | data formatting | bytes 2097152
  80.7 0.0 copy-done
  80.7 1.1 %copy.17 = f32[512,768]{1,0:T(8,128)} copy(f32[512,768]{1,0:T(8,128)S(1)} %copy-done) | data formatting | bytes 3145728
Async XLA Ops:
  77.1 3.6 %copy-start = (f32[512,768]{1,0:T(8,128)S(1)}, f32[512,768]{1,0:T(8,128)}, u32[]{:S(2)}) copy-start(f32[512,768]{1,0:T(8,128)} %get-tuple-element.13) | copy-start | bytes 4718596

commit v2 on v1

--- a/solution.py
+++ b/solution.py
@@ -24,8 +24,8 @@
 def kernel(
     n_fsdp, n_rep,
     hid_hbm, og_hbm, sav_hbm, lse_hbm, wq_hbm, wo_hbm, len_ref, start_ref, freq_ref,
-    ig_hbm, gu_hbm, norm_ref,
-    hid, og, sav, lse, wq, wo, hid_t, og_t, proj, ag, dqkv, ig, gu,
+    ig_hbm, gr_hbm, norm_ref, factor_ref,
+    hid, og, sav, lse, wq, wo, hid_t, og_t, proj, ag, dqkv, ig,
     part, core_in, rs_in, z_mid, z_in, fin, norms, tab,
     load_sem, out_sem,
     wq_send, wq_recv, wo_send, wo_recv, wqc_send, wqc_recv, woc_send, woc_recv,
@@ -39,7 +39,9 @@
     nb = n_fsdp.bit_length() - 1
     seq = hid.shape[0]
     chunks, _, _, half, cw = part.shape
-    heads = lse.shape[1]
+    heads = lse.shape[0]
+    pieces = fin_send.shape[1]
+    hp = half // pieces
     qw = heads * HEAD
     wr = 2 * half
     scale = 1.0 / HEAD**0.5
@@ -62,7 +64,7 @@
         bit *= 2
     barrier = pltpu.get_barrier_semaphore()
     greet = [partner]
-    greet += [((f + k) % n_fsdp, r) for k in range(1, n_fsdp)]
+    greet += [((f + k) % n_fsdp, 2 * z + side) for k in range(1, n_fsdp) for side in range(2)]
     greet += [(f, 2 * peer + core) for peer in [z_near, z_mirror] + z_far]
     for peer in greet:
         pl.semaphore_signal(barrier, inc=1, device_id=peer, device_id_type=MESH)
@@ -132,99 +134,130 @@
             part[chunk, 1 - core, g] = dot(left_t[g, 1 - core], right, 1, 0).astype(BF16)
         go(remote(part.at[chunk, 1 - core], core_in.at[chunk], core_send.at[chunk], core_recv.at[chunk], partner))
 
-    def rs_copy(chunk, mask):
+    def rows_of(p):
+        return pl.ds(p * hp, hp)
+
+    def rs_copy(chunk, p, mask):
         low = (mask & -mask).bit_length() - 1
-        g = block_of(mask)
         return remote(
-            part.at[chunk, core, g], rs_in.at[chunk, mask], rs_send.at[chunk, mask], rs_recv.at[chunk, mask], near[low]
+            part.at[chunk, core, block_of(mask), rows_of(p)],
+            rs_in.at[chunk, mask, rows_of(p)],
+            rs_send.at[chunk, p, mask],
+            rs_recv.at[chunk, p, mask],
+            near[low],
         )
 
-    def own_half(chunk, left_t, right):
+    def own_half(chunk, left_t, right, send=True):
         remote(
             part.at[chunk, 1 - core], core_in.at[chunk], core_send.at[chunk], core_recv.at[chunk], partner
         ).wait_recv()
-        order = sorted(range(n_fsdp), key=lambda m: 1 - m % 2)
-        for mask in order:
+
+        def term(mask):
             g = block_of(mask)
             part[chunk, core, g] = (dot(left_t[g, core], right, 1, 0) + core_in[chunk, g].astype(F32)).astype(BF16)
-            if mask & 1:
-                go(rs_copy(chunk, mask))
-
-    def rs_stage(chunk, s):
+
+        for mask in range(n_fsdp - 1, 0, -2):
+            term(mask)
+        if send:
+            send_first(chunk)
+        for mask in range(n_fsdp - 2, -1, -2):
+            term(mask)
+
+    def send_first(chunk):
+        for p in range(pieces):
+            for mask in range(n_fsdp - 1, 0, -2):
+                go(rs_copy(chunk, p, mask))
+
+    def rs_stage(chunk, p, s):
         later = [m for m in range(n_fsdp) if m % (1 << (s + 1)) == 0]
         later = sorted(later, key=lambda m: 1 - (m >> (s + 1)) % 2)
         for mask in later:
             message = mask | (1 << s)
-            rs_copy(chunk, message).wait_recv()
+            rs_copy(chunk, p, message).wait_recv()
             g = block_of(mask)
-            part[chunk, core, g] = (part[chunk, core, g].astype(F32) + rs_in[chunk, message].astype(F32)).astype(BF16)
+            at = rows_of(p)
+            part[chunk, core, g, at] = (
+                part[chunk, core, g, at].astype(F32) + rs_in[chunk, message, at].astype(F32)
+            ).astype(BF16)
             if (mask >> (s + 1)) & 1:
-                go(rs_copy(chunk, mask))
+                go(rs_copy(chunk, p, mask))
 
     middle = ((z % 4) + 1) // 2 % 2 == 1
     z_dev = [(f, 2 * peer + core) for peer in [z_near, z_mirror] + z_far]
 
-    def z_up(chunk):
-        return remote(part.at[chunk, core, f], z_in.at[chunk, 0], z_send.at[chunk, 0], z_recv.at[chunk, 0], z_dev[0])
-
-    def z_across(chunk, k):
-        return remote(
-            z_mid.at[chunk, k], z_in.at[chunk, k + 1], z_send.at[chunk, k + 1], z_recv.at[chunk, k + 1], z_dev[k + 1]
-        )
+    def z_copy(chunk, p, k, src, dst, device):
+        return remote(src, dst, z_send.at[chunk, p, k], z_recv.at[chunk, p, k], device)
+
+    def z_up(chunk, p):
+        at = rows_of(p)
+        return z_copy(chunk, p, 0, part.at[chunk, core, f, at], z_in.at[chunk, 0, at], z_dev[0])
+
+    def z_across(chunk, p, k):
+        at = rows_of(p)
+        return z_copy(chunk, p, k + 1, z_mid.at[chunk, k, at], z_in.at[chunk, k + 1, at], z_dev[k + 1])
 
     n_across = 1 + len(z_far)
 
-    def z_down(chunk):
-        k = n_across + 1
-        return remote(fin.at[chunk, core], fin.at[chunk, core], z_send.at[chunk, k], z_recv.at[chunk, k], z_dev[0])
-
-    def fin_copy(chunk):
-        return remote(fin.at[chunk, core], fin.at[chunk, core], fin_send.at[chunk], fin_recv.at[chunk], partner)
-
-    def fin_from_partner(chunk):
-        return remote(fin.at[chunk, 1 - core], fin.at[chunk, 1 - core], fin_send.at[chunk], fin_recv.at[chunk], partner)
-
-    def z_first(chunk):
+    def z_down(chunk, p):
+        ref = fin.at[chunk, core, rows_of(p)]
+        return z_copy(chunk, p, n_across + 1, ref, ref, z_dev[0])
+
+    def fin_copy(chunk, p, side):
+        ref = fin.at[chunk, side, rows_of(p)]
+        return remote(ref, ref, fin_send.at[chunk, p], fin_recv.at[chunk, p], partner)
+
+    def z_first(chunk, p):
+        at = rows_of(p)
+
         @pl.when(middle)
         def _():
-            z_up(chunk).wait_recv()
-            z_mid[chunk, 0] = (part[chunk, core, f].astype(F32) + z_in[chunk, 0].astype(F32)).astype(BF16)
-            z_across(chunk, 0).start()
-
+            z_up(chunk, p).wait_recv()
+            z_mid[chunk, 0, at] = (part[chunk, core, f, at].astype(F32) + z_in[chunk, 0, at].astype(F32)).astype(BF16)
+            z_across(chunk, p, 0).start()
+
+    def z_start(chunk, p):
         @pl.when(jnp.logical_not(middle))
         def _():
-            z_up(chunk).start()
-
-    def z_second(chunk):
+            z_up(chunk, p).start()
+
+    def z_second(chunk, p):
+        at = rows_of(p)
+
         @pl.when(middle)
         def _():
             for k in range(n_across):
-                z_across(chunk, k).wait_recv()
-                total = (z_mid[chunk, k].astype(F32) + z_in[chunk, k + 1].astype(F32)).astype(BF16)
+                z_across(chunk, p, k).wait_recv()
+                total = (z_mid[chunk, k, at].astype(F32) + z_in[chunk, k + 1, at].astype(F32)).astype(BF16)
                 if k + 1 < n_across:
-                    z_mid[chunk, k + 1] = total
-                    z_across(chunk, k + 1).start()
+                    z_mid[chunk, k + 1, at] = total
+                    z_across(chunk, p, k + 1).start()
                 else:
-                    fin[chunk, core] = total
-            z_down(chunk).start()
-
-    def z_third(chunk):
+                    fin[chunk, core, at] = total
+            z_down(chunk, p).start()
+
+    squares = [jnp.zeros((8, cw), F32)]
+
+    def z_third(chunk, p):
         @pl.when(jnp.logical_not(middle))
         def _():
-            z_down(chunk).wait_recv()
-
-        go(fin_copy(chunk))
-
-    def z_drain(chunk):
+            z_down(chunk, p).wait_recv()
+
+        go(fin_copy(chunk, p, core))
+        own = fin[chunk, core, rows_of(p)].astype(F32)
+        squares[0] = squares[0] + jnp.sum((own * own).reshape(hp // 8, 8, cw), axis=0)
+
+    def z_drain(chunk, p):
         @pl.when(middle)
         def _():
             for k in range(n_across):
-                z_across(chunk, k).wait_send()
-            z_down(chunk).wait_send()
+                z_across(chunk, p, k).wait_send()
+            z_down(chunk, p).wait_send()
 
         @pl.when(jnp.logical_not(middle))
         def _():
-            z_up(chunk).wait_send()
+            z_up(chunk, p).wait_send()
+
+    every = range(pieces)
 
     half_for_partner(0, og_t, sav[...])
     loads[4].wait()
@@ -274,9 +307,11 @@
         arrive(mask)
     for mask in range(1, last):
         use(mask)
-    own_half(0, og_t, sav[...])
+    own_half(0, og_t, sav[...], False)
     arrive(last)
+    send_first(0)
     use(last)
+    lse_rows = jnp.concatenate([lse[...]] * (8 // heads), axis=0).T
 
     queries = [rot(proj[:, h * HEAD : (h + 1) * HEAD], 1.0).astype(BF16) for h in range(heads)]
     keys = rot(proj[:, qw : qw + HEAD], 1.0).astype(BF16)
@@ -298,7 +333,7 @@
     for h in range(heads):
         lanes_h = slice(h * HEAD, (h + 1) * HEAD)
         scores = dot(queries[h], keys, 1, 1) * scale
-        probs = jnp.where(allowed, jnp.exp(scores - lse[:, h : h + 1]), 0.0)
+        probs = jnp.where(allowed, jnp.exp(scores - lse_rows[:, h : h + 1]), 0.0)
         grad_head = ag[:, lanes_h].astype(BF16)
         dprobs = dot(grad_head, values, 1, 1)
         delta = jnp.sum(grad_head.astype(F32) * sav[:, lanes_h].astype(F32), axis=1, keepdims=True)
@@ -306,8 +341,6 @@
         value_grad = value_grad + dot(probs.astype(BF16), grad_head, 0, 0)
         key_grad = key_grad + dot(dscores, queries[h], 0, 0)
         dqkv[:, lanes_h] = rot(dot(dscores, keys, 1, 0), -1.0).astype(BF16)
-        if h < nb:
-            rs_stage(0, h)
     dqkv[:, qw : qw + HEAD] = rot(key_grad, -1.0).astype(BF16)
     dqkv[:, qw + HEAD :] = value_grad.astype(BF16)
 
@@ -315,64 +348,91 @@
     right_of = {c: dqkv[:, (c - 1) * cw : c * cw] for c in rest}
     for c in rest:
         half_for_partner(c, hid_t, right_of[c])
+    for p in every:
+        rs_stage(0, p, 0)
     for c in rest:
         own_half(c, hid_t, right_of[c])
-    for s in range(heads, nb):
-        rs_stage(0, s)
-    z_first(0)
+    for s in range(1, nb):
+        for p in every:
+            rs_stage(0, p, s)
+    for p in every:
+        z_start(0, p)
 
     def grad_block(g):
         columns = slice(g * wr, (g + 1) * wr)
         ig[:, columns] = dot(dqkv[...], wq[g].reshape(wr, -1), 1, 1).astype(BF16)
 
-    for g in range(n_fsdp // 2):
-        grad_block(g)
-    z_second(0)
-    for g in range(n_fsdp // 2, n_fsdp):
-        grad_block(g)
     ig_out = pltpu.make_async_copy(ig, ig_hbm, out_sem.at[0])
-    ig_out.start()
-    z_third(0)
-    for s in range(nb):
-        for c in rest:
-            rs_stage(c, s)
+    items = [(c, p) for c in rest for p in every]
+    depth = nb + 3
+
+    def advance(c, p, s):
+        if s < nb:
+            rs_stage(c, p, s)
             if s == nb - 1:
-                z_first(c)
-    for c in rest:
-        z_second(c)
-    for c in rest:
-        z_third(c)
-
-    squares = jnp.zeros((half, cw), F32)
+                z_start(c, p)
+        elif s == nb:
+            z_first(c, p)
+        elif s == nb + 1:
+            z_second(c, p)
+        else:
+            z_third(c, p)
+
+    for t in range(len(items) + depth - 1):
+        if t < n_fsdp:
+            grad_block(t)
+        if t == n_fsdp - 1:
+            ig_out.start()
+        if t < 3:
+            for p in every:
+                advance(0, p, nb + t)
+        for k in range(max(0, t - depth + 1), min(t, len(items) - 1) + 1):
+            advance(*items[k], t - k)
+    for t in range(len(items) + depth - 1, n_fsdp):
+        grad_block(t)
+    if n_fsdp > len(items) + depth - 1:
+        ig_out.start()
+
+    mine = jnp.sum(jnp.sum(squares[0], axis=0, keepdims=True), axis=1, keepdims=True)
+    slot = 2 * f + core
+    norms[slot] = jnp.broadcast_to(mine, norms.shape[1:])
+    rounds = [(k, side) for k in range(n_fsdp) for side in range(2) if k or side]
+
+    def norm_copy(k, side, place, sign):
+        at = 2 * k + side
+        column = (f + sign * k + n_fsdp) % n_fsdp
+        row = 2 * z + (core + side) % 2
+        return remote(norms.at[place], norms.at[place], norm_send.at[at], norm_recv.at[at], (column, row))
+
+    for k, side in rounds:
+        go(norm_copy(k, side, slot, 1))
+    gr_outs = []
     for c in range(chunks):
-        fin_from_partner(c).wait_recv()
-        low, high = fin[c, 0].astype(F32), fin[c, 1].astype(F32)
-        squares = squares + low * low + high * high
-    mine = jnp.sum(jnp.sum(squares, axis=0, keepdims=True), axis=1, keepdims=True)
-    norms[f] = jnp.broadcast_to(mine, norms.shape[1:])
-    for k in range(1, n_fsdp):
-        go(remote(norms.at[f], norms.at[f], norm_send.at[k], norm_recv.at[k], ((f + k) % n_fsdp, r)))
-    for k in range(1, n_fsdp):
-        origin = (f + n_fsdp - k) % n_fsdp
-        remote(norms.at[origin], norms.at[origin], norm_send.at[k], norm_recv.at[k], (origin, r)).wait_recv()
+        for p in every:
+            fin_copy(c, p, 1 - core).wait_recv()
+        for side in range(2):
+            columns = pl.ds((c - 1) % chunks * cw, cw)
+            out = pltpu.make_async_copy(
+                fin.at[c, side], gr_hbm.at[pl.ds(side * half, half), columns], out_sem.at[1 + 2 * c + side]
+            )
+            out.start()
+            gr_outs.append(out)
+    for k, side in rounds:
+        norm_copy(k, side, 2 * ((f - k + n_fsdp) % n_fsdp) + (core + side) % 2, -1).wait_recv()
     total = norms[0]
-    for g in range(1, n_fsdp):
-        total = total + norms[g]
-    norm_ref[...] = jnp.sqrt(total)
+    for k in range(1, 2 * n_fsdp):
+        total = total + norms[k]
     size = n_fsdp * wr * chunks * cw
-    factor = lax.rsqrt(total[0:1, 0:1] / size + 1e-06)
-    for c in range(chunks):
-        at = (c - 1) % chunks * cw
-        for side in range(2):
-            gu[side * half : (side + 1) * half, at : at + cw] = fin[c, side].astype(F32) * factor
-    gu_out = pltpu.make_async_copy(gu, gu_hbm, out_sem.at[1])
-    gu_out.start()
+    norm_ref[0, 0] = jnp.max(jnp.sqrt(total))
+    factor_ref[0, 0] = jnp.max(lax.rsqrt(total / size + 1e-06))
     for copy in sent:
         copy.wait_send()
     for c in range(chunks):
-        z_drain(c)
+        for p in every:
+            z_drain(c, p)
     ig_out.wait()
-    gu_out.wait()
+    for out in gr_outs:
+        out.wait()
 
 
 def solution(mesh):
@@ -386,26 +446,28 @@
         chunks = 1 + cols // cw
         n_across = (n_rep // 2).bit_length() - 2
         lane = np.arange(HEAD) % (HEAD // 2)
-        freq = np.broadcast_to((1000000.0 ** (-2.0 * lane / HEAD)).astype(np.float32), (8, HEAD))
+        freq = np.broadcast_to((1000000.0 ** (-2.0 * lane / HEAD)).astype(np.float32), (1, HEAD))
         dma = pltpu.SemaphoreType.DMA
         anywhere = pl.BlockSpec(memory_space=pl.ANY)
         scalar = pl.BlockSpec(memory_space=pltpu.SMEM)
         vmem = pl.BlockSpec(memory_space=pltpu.VMEM)
         F = n_fsdp
-        ig, gu, norm = pl.pallas_call(
+        pieces = 4
+        ig, grads, norm, factor = pl.pallas_call(
             functools.partial(kernel, n_fsdp, n_rep),
             out_shape=(
                 jax.ShapeDtypeStruct((seq, width), BF16),
-                jax.ShapeDtypeStruct((wr, chunks * cw), F32),
-                jax.ShapeDtypeStruct((8, 128), F32),
+                jax.ShapeDtypeStruct((wr, chunks * cw), BF16),
+                jax.ShapeDtypeStruct((1, 1), F32),
+                jax.ShapeDtypeStruct((1, 1), F32),
             ),
             in_specs=[anywhere] * 6 + [scalar] * 2 + [vmem],
-            out_specs=(anywhere, anywhere, vmem),
+            out_specs=(anywhere, anywhere, scalar, scalar),
             scratch_shapes=[
                 pltpu.VMEM((seq, width), BF16),
                 pltpu.VMEM((seq, width), BF16),
                 pltpu.VMEM((seq, qw), BF16),
-                pltpu.VMEM(row_lse.shape, F32),
+                pltpu.VMEM(row_lse.shape[::-1], F32),
                 pltpu.VMEM((F, 2, half, cols), BF16),
                 pltpu.VMEM((F, 2, half, qw), BF16),
                 pltpu.VMEM((F, 2, half, seq), BF16),
@@ -414,33 +476,32 @@
                 pltpu.VMEM((seq, qw), F32),
                 pltpu.VMEM((seq, cols), BF16),
                 pltpu.VMEM((seq, width), BF16),
-                pltpu.VMEM((wr, chunks * cw), F32),
                 pltpu.VMEM((chunks, 2, F, half, cw), BF16),
                 pltpu.VMEM((chunks, F, half, cw), BF16),
                 pltpu.VMEM((chunks, F, half, cw), BF16),
                 pltpu.VMEM((chunks, n_across, half, cw), BF16),
                 pltpu.VMEM((chunks, n_across + 1, half, cw), BF16),
                 pltpu.VMEM((chunks, 2, half, cw), BF16),
-                pltpu.VMEM((F, 8, 128), F32),
+                pltpu.VMEM((2 * F, 8, 128), F32),
                 pltpu.VMEM((2, seq, HEAD), F32),
                 dma((6,)),
-                dma((2,)),
+                dma((1 + 2 * chunks,)),
             ]
             + [dma((F,))] * 8
             + [dma((chunks,))] * 2
-            + [dma((chunks, F))] * 2
-            + [dma((chunks, n_across + 2))] * 2
-            + [dma((chunks,))] * 2
-            + [dma((F,))] * 2,
+            + [dma((chunks, pieces, F))] * 2
+            + [dma((chunks, pieces, n_across + 2))] * 2
+            + [dma((chunks, pieces))] * 2
+            + [dma((2 * F,))] * 2,
             compiler_params=pltpu.CompilerParams(
                 collective_id=0, has_side_effects=True, vmem_limit_bytes=56 * 2**20
             ),
         )(
-            hidden_in, out_grad, attn_saved, row_lse,
+            hidden_in, out_grad, attn_saved, row_lse.T,
             w_qkv.reshape(2, half, cols), w_out_t.reshape(2, half, qw),
             doc_lengths, seq_start, freq,
         )
-        return ig, gu, norm[0, 0]
+        return ig, grads.astype(F32) * factor[0, 0], norm[0, 0]
 
     rows = P(("fsdp", "rep"), None)
     in_specs = (rows, rows, rows, rows, P("fsdp", None), P("fsdp", None), rows, P(("fsdp", "rep")))

time: 82.1 us -> 82.7 us (level)
  local copies, waits for them, and re-layouts: 7.48 us -> 0.97 us
  other arithmetic: 0 us -> 3.1 us
  Pallas kernels: 73 us -> 75.3 us
  between operations: 1.3 us -> 3.11 us
    unnamed x5 -> x3, local copies, waits for them, and re-layouts: 4.93 us -> 0.97 us
    mul x0 -> x1, other arithmetic: none -> 3.1 us  [body(): return (ig, grads.astype(F32) * factor[0, 0], norm[0, 0])]
    pallas_call x1, Pallas kernels: 73 us -> 75.3 us  [body(): pl.pallas_call(functools.partial(kernel, n_fsdp, n_rep), out_shape=(jax.S...]
    slice x1 -> x0, local copies, waits for them, and re-layouts: 1.31 us -> none  [body(): return (ig, gu, norm[0, 0])]
    another operation x1 -> x0, local copies, waits for them, and re-layouts: 1.25 us -> none
where the time goes in v2:
time: 82.7 us; the launch traced here: 82.5 us
  Pallas kernels  75.3 us (91%)
  between operations  3.11 us (4%)
  other arithmetic  3.1 us (4%)
  local copies, waits for them, and re-layouts  0.97 us (1%)
    pallas_call x1, Pallas kernels, body(): pl.pallas_call(functools.partial(kernel, n_fsdp, n_rep), out_shape=(jax.S...  75.3 us
    mul x1, other arithmetic, body(): return (ig, grads.astype(F32) * factor[0, 0], norm[0, 0])  3.1 us

profile of v2, /device:TPU:0, one launch (start us, length us, event | category | flops | bytes accessed | tf_op | source)
XLA Modules:
  0.0 82.5 jit_solution(8207633885923784432)
XLA Ops:
  1.3 75.3 %shard_map.112 = (bf16[256,2048]{1,0:T(8,128)(2,1)}, bf16[512,768]{1,0:T(8,128)(2,1)}, f32[1,1]{1,0:T(1,128)}, f32[1,1]{1,0:T(1,128)}) custom-call(bf16[256,2048]{1,0:T(8,128)(2,1)} %hid_hbm.1, bf16[256,2048]{1,0:T(8,128)(2,1)} %og_hbm.1, bf16[256,256]{1,0:T(8,128)(2,1)} %sav_hbm.1, f32[2,256]{1,0:T(2,128)} %bitcast.7, bf16[2,256,512]{2,1,0:T(8,128)(2,1)} %bitcast.5, ...), custom_call_target="tpu_custom_call" | custom-call | tf_op jit(solution)/shard_map/pallas_call | solution.py:456
  76.6 0.0 copy-start
  76.6 3.1 %convert_multiply_fusion = f32[512,768]{1,0:T(8,128)} fusion(bf16[512,768]{1,0:T(8,128)(2,1)} %get-tuple-element.8, f32[]{:T(128)} %bitcast.3), kind=kLoop, calls=%fused_computation | loop fusion | flops 786432 | bytes 2359300 | tf_op jit(solution)/shard_map/mul | solution.py:504
  79.7 0.0 copy-done
  79.7 1.0 %copy.15 = bf16[256,2048]{1,0:T(8,128)(2,1)} copy(bf16[256,2048]{1,0:T(8,128)(2,1)S(1)} %copy-done) | data formatting | bytes 2097152
Async XLA Ops:
  76.6 3.1 %copy-start = (bf16[256,2048]{1,0:T(8,128)(2,1)S(1)}, bf16[256,2048]{1,0:T(8,128)(2,1)}, u32[]{:S(2)}) copy-start(bf16[256,2048]{1,0:T(8,128)(2,1)} %get-tuple-element.14) | copy-start | bytes 3145732

commit v3 on v2

--- a/solution.py
+++ b/solution.py
@@ -378,7 +378,7 @@
         else:
             z_third(c, p)
 
-    for t in range(len(items) + depth - 1):
+    for t in range(depth):
         if t < n_fsdp:
             grad_block(t)
         if t == n_fsdp - 1:
@@ -386,11 +386,11 @@
         if t < 3:
             for p in every:
                 advance(0, p, nb + t)
-        for k in range(max(0, t - depth + 1), min(t, len(items) - 1) + 1):
-            advance(*items[k], t - k)
-    for t in range(len(items) + depth - 1, n_fsdp):
+        for c, p in items:
+            advance(c, p, t)
+    for t in range(depth, n_fsdp):
         grad_block(t)
-    if n_fsdp > len(items) + depth - 1:
+    if n_fsdp > depth:
         ig_out.start()
 
     mine = jnp.sum(jnp.sum(squares[0], axis=0, keepdims=True), axis=1, keepdims=True)
@@ -452,7 +452,7 @@
         scalar = pl.BlockSpec(memory_space=pltpu.SMEM)
         vmem = pl.BlockSpec(memory_space=pltpu.VMEM)
         F = n_fsdp
-        pieces = 4
+        pieces = 2
         ig, grads, norm, factor = pl.pallas_call(
             functools.partial(kernel, n_fsdp, n_rep),
             out_shape=(

time: 82.7 us -> 65.1 us (0.79)
  Pallas kernels: 75.3 us -> 57.7 us
    pallas_call x1, Pallas kernels: 75.3 us -> 57.7 us  [body(): pl.pallas_call(functools.partial(kernel, n_fsdp, n_rep), out_shape=(jax.S...]
where the time goes in v3:
time: 65.1 us; the launch traced here: 64.9 us
  Pallas kernels  57.7 us (89%)
  between operations  3.11 us (5%)
  other arithmetic  3.1 us (5%)
  local copies, waits for them, and re-layouts  0.97 us (1%)
    pallas_call x1, Pallas kernels, body(): pl.pallas_call(functools.partial(kernel, n_fsdp, n_rep), out_shape=(jax.S...  57.7 us
    mul x1, other arithmetic, body(): return (ig, grads.astype(F32) * factor[0, 0], norm[0, 0])  3.1 us

profile of v3, /device:TPU:0, one launch (start us, length us, event | category | flops | bytes accessed | tf_op | source)
XLA Modules:
  0.0 64.9 jit_solution(4040301761915660722)
XLA Ops:
  1.3 57.7 %shard_map.112 = (bf16[256,2048]{1,0:T(8,128)(2,1)}, bf16[512,768]{1,0:T(8,128)(2,1)}, f32[1,1]{1,0:T(1,128)}, f32[1,1]{1,0:T(1,128)}) custom-call(bf16[256,2048]{1,0:T(8,128)(2,1)} %hid_hbm.1, bf16[256,2048]{1,0:T(8,128)(2,1)} %og_hbm.1, bf16[256,256]{1,0:T(8,128)(2,1)} %sav_hbm.1, f32[2,256]{1,0:T(2,128)} %bitcast.7, bf16[2,256,512]{2,1,0:T(8,128)(2,1)} %bitcast.5, ...), custom_call_target="tpu_custom_call" | custom-call | tf_op jit(solution)/shard_map/pallas_call | solution.py:456
  59.0 0.0 copy-start
  59.0 3.1 %convert_multiply_fusion = f32[512,768]{1,0:T(8,128)} fusion(bf16[512,768]{1,0:T(8,128)(2,1)} %get-tuple-element.8, f32[]{:T(128)} %bitcast.3), kind=kLoop, calls=%fused_computation | loop fusion | flops 786432 | bytes 2359300 | tf_op jit(solution)/shard_map/mul | solution.py:504
  62.1 0.0 copy-done
  62.1 1.0 %copy.15 = bf16[256,2048]{1,0:T(8,128)(2,1)} copy(bf16[256,2048]{1,0:T(8,128)(2,1)S(1)} %copy-done) | data formatting | bytes 2097152
Async XLA Ops:
  59.0 3.1 %copy-start = (bf16[256,2048]{1,0:T(8,128)(2,1)S(1)}, bf16[256,2048]{1,0:T(8,128)(2,1)}, u32[]{:S(2)}) copy-start(bf16[256,2048]{1,0:T(8,128)(2,1)} %get-tuple-element.14) | copy-start | bytes 3145732
